TPU v7x, 128 devices: a whole 4x4x4 slice. The times are simulated.
128 devices in a mesh: expert: 4 (over x_lo, core), shard: 32 (over z, y, x_hi).
Axes of the slice: x: 4 (x_hi: 2, x_lo: 2; x = x_hi * 2 + x_lo), y: 4, z: 4, core: 2. Of those that a mesh axis runs over, the one named last changes fastest.
Arguments:
- master_gate: float32 [64, 2048, 1024], P('expert', 'shard'), may hold values from -0.25 to 0.25
- second_gate: bfloat16 [64, 2048, 1024], P('expert', 'shard'), may hold values from -0.0625 to 0.0625
- master_up: float32 [64, 2048, 1024], P('expert', 'shard'), may hold values from -0.25 to 0.25
- second_up: bfloat16 [64, 2048, 1024], P('expert', 'shard'), may hold values from -0.0625 to 0.0625
- master_down: float32 [64, 1024, 2048], P('expert', None, 'shard'), may hold values from -0.375 to 0.375
- second_down: bfloat16 [64, 1024, 2048], P('expert', None, 'shard'), may hold values from -0.09375 to 0.09375
- router_weight: float32 [2048, 64], P('shard', 'expert'), may hold values from -0.125 to 0.125
- router_gain: float32 [2048], P('shard'), may hold values from 0.25 to 1.75
Outputs:
- final_gate: bfloat16 [64, 2048, 1024], P('expert', None, 'shard')
- final_up: bfloat16 [64, 2048, 1024], P('expert', None, 'shard')
- final_down: bfloat16 [64, 1024, 2048], P('expert', 'shard')
- scale_gate: float32 [64, 1024], P('expert', 'shard')
- scale_up: float32 [64, 1024], P('expert', 'shard')
- scale_down: float32 [64, 1024], P('expert', 'shard')
- serve_router: bfloat16 [2048, 64], replicated
All inputs are finite; a program needn't handle non-finite values. Where the computation divides by a largest or mean magnitude, that divisor is 1e-20 or more.
Results may differ from a plain program's by a relative error of at most 0.001.
Values may be sent and summed in bfloat16 or wider, within the bound.
A program may use at most 128 MiB of HBM per device.

v0:
```python
import jax
import jax.numpy as jnp
from jax import lax
from jax.sharding import PartitionSpec as P


def over_pieces(array, axis):
    blocks = lax.all_gather(array, axis)
    return blocks.max(axis=0)


def joined_along(blocks, dim):
    blocks = jnp.moveaxis(blocks, 0, dim)
    lengths = blocks.shape
    return blocks.reshape(*lengths[:dim], lengths[dim] * lengths[dim + 1], *lengths[dim + 2 :])


def copy_for_each(array, axis):
    copies = jnp.broadcast_to(array, (lax.axis_size(axis), *array.shape))
    return lax.all_to_all(copies, axis, split_axis=0, concat_axis=0, tiled=True)


def gather_directly(array, axis, dim):
    return joined_along(copy_for_each(array, axis), dim)


def per_device(
    master_gate,
    second_gate,
    master_up,
    second_up,
    master_down,
    second_down,
    router_weight,
    router_gain,
):
    merged_gate = master_gate + second_gate.astype(jnp.float32)
    merged_up = master_up + second_up.astype(jnp.float32)
    merged_down = master_down + second_down.astype(jnp.float32)
    scale_gate, scale_up, scale_down = (
        over_pieces(jnp.max(jnp.abs(merged_gate), axis=1), "shard"),
        over_pieces(jnp.max(jnp.abs(merged_up), axis=1), "shard"),
        over_pieces(jnp.max(jnp.abs(merged_down), axis=2), "shard"),
    )
    narrow_gate, narrow_up, narrow_down = (
        (merged_gate / jnp.expand_dims(scale_gate, 1)).astype(jnp.bfloat16),
        (merged_up / jnp.expand_dims(scale_up, 1)).astype(jnp.bfloat16),
        (merged_down / jnp.expand_dims(scale_down, 2)).astype(jnp.bfloat16),
    )
    final_gate, final_up = (
        lax.all_to_all(narrow_gate, "shard", split_axis=2, concat_axis=1, tiled=True),
        lax.all_to_all(narrow_up, "shard", split_axis=2, concat_axis=1, tiled=True),
    )
    final_down = lax.all_to_all(narrow_down, "shard", split_axis=1, concat_axis=2, tiled=True)
    scale_gate = lax.dynamic_slice_in_dim(
        scale_gate, lax.axis_index("shard") * final_gate.shape[2], final_gate.shape[2], axis=1
    )
    scale_up = lax.dynamic_slice_in_dim(
        scale_up, lax.axis_index("shard") * final_up.shape[2], final_up.shape[2], axis=1
    )
    scale_down = lax.dynamic_slice_in_dim(
        scale_down, lax.axis_index("shard") * final_down.shape[1], final_down.shape[1], axis=1
    )
    part_router = (router_weight * router_gain[:, None]).astype(jnp.bfloat16)
    row_router = gather_directly(part_router, "shard", 0)
    serve_router = gather_directly(row_router, "expert", 1)
    return (final_gate, final_up, final_down, scale_gate, scale_up, scale_down, serve_router)


def solution(mesh):
    in_specs = (
        P("expert", "shard", None),
        P("expert", "shard", None),
        P("expert", "shard", None),
        P("expert", "shard", None),
        P("expert", None, "shard"),
        P("expert", None, "shard"),
        P("shard", "expert"),
        P("shard"),
    )
    out_specs = (
        P("expert", None, "shard"),
        P("expert", None, "shard"),
        P("expert", "shard", None),
        P("expert", "shard"),
        P("expert", "shard"),
        P("expert", "shard"),
        P(),
    )
    return jax.shard_map(
        per_device, mesh=mesh, in_specs=in_specs, out_specs=out_specs, check_vma=False
    )
```

profile of v0, /device:TPU:6, one launch (start us, length us, event | category | flops | bytes accessed | tf_op | source)
XLA Modules:
  0.0 352.2 jit_solution(11286700278686036596)
XLA Ops:
  7.2 0.0 copy-start.1
  7.2 0.0 all-gather.7.cloned.1.call-start
  7.2 4.4 %abs_reduce_fusion.2 = f32[16,1024]{1,0:T(8,128)} fusion(f32[16,64,1024]{2,1,0:T(8,128)} %param.8, bf16[16,64,1024]{2,1,0:T(8,128)(2,1)} %param.9), kind=kLoop, calls=%fused_computation.7 | loop fusion | flops 4177920 | bytes 6356992 | tf_op jit(solution)/shard_map/reduce_max | solution.py:41
  11.6 0.0 copy-start.2
  11.6 0.0 copy-start.3
  11.6 0.0 all-gather.7.cloned.1.call-update
  11.7 0.0 all-gather.9.cloned.1.call-start
  11.7 0.0 copy-done.1
  11.7 3.6 %abs_reduce_fusion.1 = f32[16,1024]{1,0:T(8,128)} fusion(f32[16,64,1024]{2,1,0:T(8,128)} %param.10, bf16[16,64,1024]{2,1,0:T(8,128)(2,1)S(1)} %copy-done.1), kind=kLoop, calls=%fused_computation.4 | loop fusion | flops 4177920 | bytes 6356992 | tf_op jit(solution)/shard_map/reduce_max | solution.py:42
  15.3 0.0 all-gather.9.cloned.1.call-update
  15.3 0.0 copy-done.2
  15.3 0.0 copy-done.3
  15.4 0.8 reshape.35
  16.2 11.1 %all-to-all-start.3 = ((bf16[32,2,512]{2,1,0:T(2,128)(2,1)}), bf16[32,2,512]{2,1,0:T(2,128)(2,1)S(1)}, u32[]{:S(2)}, u32[]{:S(2)}) async-start(bf16[32,2,512]{2,1,0:T(2,128)(2,1)} %reshape.35), calls=%async_computation.3 | async-start | bytes 131072 | tf_op jit(solution)/shard_map/all_to_all | solution.py:20
  27.2 0.0 copy-start
  27.2 0.0 all-gather.11.cloned.1.call-start
  27.3 4.4 %abs_reduce_fusion = f32[16,1024]{1,0:T(8,128)} fusion(f32[16,1024,64]{1,2,0:T(8,128)} %param.12, bf16[16,1024,64]{1,2,0:T(8,128)(2,1)} %param.13), kind=kLoop, calls=%fused_computation.1 | loop fusion | flops 4177920 | bytes 6356992 | tf_op jit(solution)/shard_map/reduce_max | solution.py:43
  31.7 0.0 all-gather.11.cloned.1.call-update
  31.7 2.8 all-to-all-done.3
  34.6 0.1 reshape.36
  34.7 0.2 reshape.24
  34.9 0.7 broadcast_in_dim.5
  35.6 4.2 %all-to-all-start.4 = ((bf16[4,2048,16]{1,2,0:T(8,128)(2,1)}), bf16[4,2048,16]{1,2,0:T(8,128)(2,1)S(1)}, u32[]{:S(2)}, u32[]{:S(2)}) async-start(bf16[4,2048,16]{1,2,0:T(8,128)(2,1)} %broadcast_in_dim.5), calls=%async_computation.4 | async-start | bytes 524288 | tf_op jit(solution)/shard_map/all_to_all | solution.py:20
  39.9 43.3 %all-gather.7.cloned.1.call-done = f32[512,1024]{1,0:T(8,128)} async-done(((f32[16,1024]{1,0:T(8,128)}), f32[512,1024]{1,0:T(8,128)}) %all-gather.7.cloned.1.call-update) | async-done | bytes 2097168 | tf_op jit(solution)/shard_map/all_gather | solution.py:8
  83.1 1.7 reduce_max.55
  84.8 0.0 copy-done
  84.8 4.4 %divide_convert_fusion.2 = bf16[16,64,1024]{2,1,0:T(8,128)(2,1)} fusion(f32[16,64,1024]{2,1,0:T(8,128)} %param.8, bf16[16,64,1024]{2,1,0:T(8,128)(2,1)S(1)} %copy-done, f32[16,1024]{1,0:T(8,128)S(1)} %reduce_max.55), kind=kLoop, calls=%fused_computation.6 | loop fusion | flops 4194304 | bytes 8454144 | tf_op jit(solution)/shard_map/convert_element_type | solution.py:46
  89.2 6.2 %copy.120 = bf16[16,64,1024]{1,0,2:T(8,128)(2,1)} copy(bf16[16,64,1024]{2,1,0:T(8,128)(2,1)} %divide_convert_fusion.2) | data formatting | bytes 4194304 | tf_op jit(solution)/shard_map/convert_element_type | solution.py:46
  95.4 7.9 %reshape.29 = bf16[32,2,16384]{2,1,0:T(2,128)(2,1)} reshape(bf16[1024,16,64]{2,1,0:T(8,128)(2,1)} %bitcast.36) | data formatting | bytes 4194304
  103.3 0.0 all-to-all-done.4
  103.3 8.6 %all-to-all-start = ((bf16[32,2,16384]{2,1,0:T(2,128)(2,1)}), bf16[32,2,16384]{2,1,0:T(2,128)(2,1)S(1)}, u32[]{:S(2)}, u32[]{:S(2)}) async-start(bf16[32,2,16384]{2,1,0:T(2,128)(2,1)} %reshape.29), calls=%async_computation | async-start | bytes 4194304 | tf_op jit(solution)/shard_map/all_to_all | solution.py:51
  111.9 55.8 %all-gather.9.cloned.1.call-done = f32[512,1024]{1,0:T(8,128)} async-done(((f32[16,1024]{1,0:T(8,128)}), f32[512,1024]{1,0:T(8,128)}) %all-gather.9.cloned.1.call-update) | async-done | bytes 2097168 | tf_op jit(solution)/shard_map/all_gather | solution.py:8
  167.7 1.7 reduce_max.57
  169.4 5.0 %divide_convert_fusion.1 = bf16[16,64,1024]{2,1,0:T(8,128)(2,1)} fusion(f32[16,64,1024]{2,1,0:T(8,128)} %param.10, bf16[16,64,1024]{2,1,0:T(8,128)(2,1)} %param.11, f32[16,1024]{1,0:T(8,128)S(1)} %reduce_max.57), kind=kLoop, calls=%fused_computation.3 | loop fusion | flops 4194304 | bytes 8454144 | tf_op jit(solution)/shard_map/convert_element_type | solution.py:47
  174.4 6.2 %copy.125 = bf16[16,64,1024]{1,0,2:T(8,128)(2,1)} copy(bf16[16,64,1024]{2,1,0:T(8,128)(2,1)} %divide_convert_fusion.1) | data formatting | bytes 4194304 | tf_op jit(solution)/shard_map/convert_element_type | solution.py:47
  180.5 7.9 %reshape.31 = bf16[32,2,16384]{2,1,0:T(2,128)(2,1)} reshape(bf16[1024,16,64]{2,1,0:T(8,128)(2,1)} %bitcast.37) | data formatting | bytes 4194304
  188.4 0.0 all-to-all-done
  188.4 8.6 %all-to-all-start.1 = ((bf16[32,2,16384]{2,1,0:T(2,128)(2,1)}), bf16[32,2,16384]{2,1,0:T(2,128)(2,1)}, u32[]{:S(2)}, u32[]{:S(2)}) async-start(bf16[32,2,16384]{2,1,0:T(2,128)(2,1)} %reshape.31), calls=%async_computation.1 | async-start | bytes 4194304 | tf_op jit(solution)/shard_map/all_to_all | solution.py:52
  197.1 55.7 %all-gather.11.cloned.1.call-done = f32[512,1024]{1,0:T(8,128)} async-done(((f32[16,1024]{1,0:T(8,128)}), f32[512,1024]{1,0:T(8,128)}) %all-gather.11.cloned.1.call-update) | async-done | bytes 2097168 | tf_op jit(solution)/shard_map/all_gather | solution.py:8
  252.8 1.7 reduce_max.59
  254.5 5.0 %divide_convert_fusion = bf16[16,1024,64]{1,2,0:T(8,128)(2,1)} fusion(f32[16,1024,64]{1,2,0:T(8,128)} %param.12, bf16[16,1024,64]{1,2,0:T(8,128)(2,1)} %param.13, f32[16,1024]{1,0:T(8,128)S(1)} %reduce_max.59), kind=kLoop, calls=%fused_computation | loop fusion | flops 4194304 | bytes 8454144 | tf_op jit(solution)/shard_map/convert_element_type | solution.py:48
  259.5 6.2 %copy.130 = bf16[16,1024,64]{2,0,1:T(8,128)(2,1)} copy(bf16[16,1024,64]{1,2,0:T(8,128)(2,1)} %divide_convert_fusion) | data formatting | bytes 4194304 | tf_op jit(solution)/shard_map/convert_element_type | solution.py:48
  265.7 7.9 %reshape.33 = bf16[32,2,16384]{2,1,0:T(2,128)(2,1)} reshape(bf16[1024,16,64]{2,1,0:T(8,128)(2,1)} %bitcast.38) | data formatting | bytes 4194304
  273.6 0.0 all-to-all-done.1
  273.6 8.6 %all-to-all-start.2 = ((bf16[32,2,16384]{2,1,0:T(2,128)(2,1)}), bf16[32,2,16384]{2,1,0:T(2,128)(2,1)}, u32[]{:S(2)}, u32[]{:S(2)}) async-start(bf16[32,2,16384]{2,1,0:T(2,128)(2,1)} %reshape.33), calls=%async_computation.2 | async-start | bytes 4194304 | tf_op jit(solution)/shard_map/all_to_all | solution.py:54
  282.2 0.7 constant_dynamic-slice_fusion
  282.9 0.7 constant_dynamic-slice_fusion.1
  283.6 0.7 constant_dynamic-slice_fusion.2
  284.3 4.0 %reshape.30 = bf16[1024,16,64]{2,1,0:T(8,128)(2,1)} reshape(bf16[32,2,16384]{2,1,0:T(2,128)(2,1)S(1)} %all-to-all-done) | data formatting | bytes 4194304
  288.2 6.9 %copy.122 = bf16[16,32,64,32]{2,1,3,0:T(8,128)(2,1)} copy(bf16[16,32,64,32]{2,0,3,1:T(8,128)(2,1)} %bitcast.39) | data formatting | bytes 4194304 | tf_op jit(solution)/shard_map/all_to_all | solution.py:51
  295.1 6.7 %all_to_all.48 = bf16[16,2048,32]{1,2,0:T(8,128)(2,1)} reshape(bf16[16,32,64,32]{2,1,3,0:T(8,128)(2,1)} %copy.122) | data formatting | bytes 4194304 | tf_op jit(solution)/shard_map/all_to_all | solution.py:51
  301.9 7.9 %reshape.32 = bf16[1024,16,64]{2,1,0:T(8,128)(2,1)} reshape(bf16[32,2,16384]{2,1,0:T(2,128)(2,1)} %all-to-all-done.1) | data formatting | bytes 4194304
  309.8 6.9 %copy.127 = bf16[16,32,64,32]{2,1,3,0:T(8,128)(2,1)} copy(bf16[16,32,64,32]{2,0,3,1:T(8,128)(2,1)} %bitcast.40) | data formatting | bytes 4194304 | tf_op jit(solution)/shard_map/all_to_all | solution.py:52
  316.6 6.7 %all_to_all.52 = bf16[16,2048,32]{1,2,0:T(8,128)(2,1)} reshape(bf16[16,32,64,32]{2,1,3,0:T(8,128)(2,1)} %copy.127) | data formatting | bytes 4194304 | tf_op jit(solution)/shard_map/all_to_all | solution.py:52
  323.4 0.0 all-to-all-done.2
  323.4 7.9 %reshape.34 = bf16[1024,16,64]{2,1,0:T(8,128)(2,1)} reshape(bf16[32,2,16384]{2,1,0:T(2,128)(2,1)} %all-to-all-done.2) | data formatting | bytes 4194304
  331.3 6.9 %copy.132 = bf16[16,32,32,64]{3,2,1,0:T(8,128)(2,1)} copy(bf16[16,32,32,64]{3,0,1,2:T(8,128)(2,1)} %bitcast.41) | data formatting | bytes 4194304 | tf_op jit(solution)/shard_map/all_to_all | solution.py:54
  338.2 6.7 %all_to_all.56 = bf16[16,32,2048]{2,1,0:T(8,128)(2,1)} reshape(bf16[16,32,32,64]{3,2,1,0:T(8,128)(2,1)} %copy.132) | data formatting | bytes 4194304 | tf_op jit(solution)/shard_map/all_to_all | solution.py:54
  344.9 0.7 copy.141
  (3 shorter events, 0.1 us)
Async XLA Ops:
  7.2 4.5 %copy-start.1 = (bf16[16,64,1024]{2,1,0:T(8,128)(2,1)S(1)}, bf16[16,64,1024]{2,1,0:T(8,128)(2,1)}, u32[]{:S(2)}) copy-start(bf16[16,64,1024]{2,1,0:T(8,128)(2,1)} %param.11) | copy-start | bytes 6291460
  7.2 75.9 %all-gather.7.cloned.1.call-start = ((), (), s32[]{:S(2)}) async-start(), calls=%async_computation.5 | async-start | bytes 2162688 | tf_op jit(solution)/shard_map/all_gather | solution.py:8
  11.6 3.7 %copy-start.2 = (f32[64,16]{0,1:T(8,128)S(1)}, f32[64,16]{0,1:T(8,128)}, u32[]{:S(2)}) copy-start(f32[64,16]{0,1:T(8,128)} %param.14) | copy-start | bytes 12292
  11.6 3.7 %copy-start.3 = (f32[64]{0:T(128)S(1)}, f32[64]{0:T(128)}, u32[]{:S(2)}) copy-start(f32[64]{0:T(128)} %param.15) | copy-start | bytes 772
  11.7 156.0 %all-gather.9.cloned.1.call-start = ((), (), s32[]{:S(2)}) async-start(), calls=%async_computation.6 | async-start | bytes 2162688 | tf_op jit(solution)/shard_map/all_gather | solution.py:8
  16.2 18.4 %all-to-all-start.3 = ((bf16[32,2,512]{2,1,0:T(2,128)(2,1)}), bf16[32,2,512]{2,1,0:T(2,128)(2,1)S(1)}, u32[]{:S(2)}, u32[]{:S(2)}) async-start(bf16[32,2,512]{2,1,0:T(2,128)(2,1)} %reshape.35), calls=%async_computation.3 | async-start | bytes 131072 | tf_op jit(solution)/shard_map/all_to_all | solution.py:20
  27.2 57.6 %copy-start = (bf16[16,64,1024]{2,1,0:T(8,128)(2,1)S(1)}, bf16[16,64,1024]{2,1,0:T(8,128)(2,1)}, u32[]{:S(2)}) copy-start(bf16[16,64,1024]{2,1,0:T(8,128)(2,1)} %param.9) | copy-start | bytes 6291460
  27.2 225.6 %all-gather.11.cloned.1.call-start = ((), (), s32[]{:S(2)}) async-start(), calls=%async_computation.7 | async-start | bytes 2162688 | tf_op jit(solution)/shard_map/all_gather | solution.py:8
  35.6 67.6 %all-to-all-start.4 = ((bf16[4,2048,16]{1,2,0:T(8,128)(2,1)}), bf16[4,2048,16]{1,2,0:T(8,128)(2,1)S(1)}, u32[]{:S(2)}, u32[]{:S(2)}) async-start(bf16[4,2048,16]{1,2,0:T(8,128)(2,1)} %broadcast_in_dim.5), calls=%async_computation.4 | async-start | bytes 524288 | tf_op jit(solution)/shard_map/all_to_all | solution.py:20
  103.3 85.2 %all-to-all-start = ((bf16[32,2,16384]{2,1,0:T(2,128)(2,1)}), bf16[32,2,16384]{2,1,0:T(2,128)(2,1)S(1)}, u32[]{:S(2)}, u32[]{:S(2)}) async-start(bf16[32,2,16384]{2,1,0:T(2,128)(2,1)} %reshape.29), calls=%async_computation | async-start | bytes 4194304 | tf_op jit(solution)/shard_map/all_to_all | solution.py:51
  188.4 85.2 %all-to-all-start.1 = ((bf16[32,2,16384]{2,1,0:T(2,128)(2,1)}), bf16[32,2,16384]{2,1,0:T(2,128)(2,1)}, u32[]{:S(2)}, u32[]{:S(2)}) async-start(bf16[32,2,16384]{2,1,0:T(2,128)(2,1)} %reshape.31), calls=%async_computation.1 | async-start | bytes 4194304 | tf_op jit(solution)/shard_map/all_to_all | solution.py:52
  273.6 49.8 %all-to-all-start.2 = ((bf16[32,2,16384]{2,1,0:T(2,128)(2,1)}), bf16[32,2,16384]{2,1,0:T(2,128)(2,1)}, u32[]{:S(2)}, u32[]{:S(2)}) async-start(bf16[32,2,16384]{2,1,0:T(2,128)(2,1)} %reshape.33), calls=%async_computation.2 | async-start | bytes 4194304 | tf_op jit(solution)/shard_map/all_to_all | solution.py:54
Sparse Core Ops, SparseCore 0:
  11.8 71.2 all-gather.6
  86.8 80.8 all-gather.8
  171.3 81.4 all-gather.10
where the time goes:
time: 354 us; the launch traced here: 352 us
  waiting for transfers between devices  158 us (45%)
  local copies, waits for them, and re-layouts  107 us (30%)
  starting transfers between devices  41.3 us (12%)
  other arithmetic  31.9 us (9%)
  between operations  13.9 us (4%)
    all_gather x3, waiting for transfers between devices, over_pieces(): blocks = lax.all_gather(array, axis)  155 us
    unnamed x18, local copies, waits for them, and re-layouts  45.1 us
    all_to_all x2, starting transfers between devices, copy_for_each(): return lax.all_to_all(copies, axis, split_axis=0, concat_axis=0, tiled=True)  15.3 us
    all_to_all x2, local copies, waits for them, and re-layouts, per_device(): lax.all_to_all(narrow_gate, 'shard', split_axis=2, concat_axis=1, tiled=T...  13.6 us
    all_to_all x2, local copies, waits for them, and re-layouts, per_device(): lax.all_to_all(narrow_down, 'shard', split_axis=1, concat_axis=2, tiled=T...  13.6 us
    all_to_all x2, local copies, waits for them, and re-layouts, per_device(): lax.all_to_all(narrow_up, 'shard', split_axis=2, concat_axis=1, tiled=True)  13.6 us
    all_to_all x1, starting transfers between devices, per_device(): lax.all_to_all(narrow_up, 'shard', split_axis=2, concat_axis=1, tiled=True)  8.64 us
    all_to_all x1, starting transfers between devices, per_device(): lax.all_to_all(narrow_down, 'shard', split_axis=1, concat_axis=2, tiled=T...  8.64 us
  transfers between devices with their start and end apart: 8, of which 4 were waited for; matrix products, arithmetic and copies ran while one was open for 28% of the time, Pallas kernels for 0%

commit v1 on v0

--- a/solution.py
+++ b/solution.py
@@ -47,8 +47,20 @@
         (merged_up / jnp.expand_dims(scale_up, 1)).astype(jnp.bfloat16),
         (merged_down / jnp.expand_dims(scale_down, 2)).astype(jnp.bfloat16),
     )
+
+    def use_lots_all(original, mesh_ax):
+        return jnp.concatenate(
+            lax.all_to_all(
+                jnp.stack(jnp.split(original, lax.axis_size(mesh_ax), axis=2)),
+                mesh_ax,
+                split_axis=0,
+                concat_axis=0,
+            ),
+            axis=1,
+        )
+
     final_gate, final_up = (
-        lax.all_to_all(narrow_gate, "shard", split_axis=2, concat_axis=1, tiled=True),
+        use_lots_all(narrow_gate, mesh_ax="shard"),
         lax.all_to_all(narrow_up, "shard", split_axis=2, concat_axis=1, tiled=True),
     )
     final_down = lax.all_to_all(narrow_down, "shard", split_axis=1, concat_axis=2, tiled=True)

time: 354 us -> 367 us (1.037)
  local copies, waits for them, and re-layouts: 107 us -> 115 us
  other arithmetic: 31.9 us -> 36.7 us
    reshape x0 -> x3, local copies, waits for them, and re-layouts: none -> 14.4 us  [use_lots_all(): jnp.concatenate(lax.all_to_all(jnp.stack(jnp.split(original, lax.axis_siz...]
    all_to_all x2 -> x0, local copies, waits for them, and re-layouts: 13.6 us -> none  [per_device(): lax.all_to_all(narrow_gate, 'shard', split_axis=2, concat_axis=1, tiled=T...]
    unnamed x18 -> x53, local copies, waits for them, and re-layouts: 45.1 us -> 57.9 us
    convert_element_type x1 -> x0, local copies, waits for them, and re-layouts: 6.17 us -> none  [per_device(): (merged_gate / jnp.expand_dims(scale_gate, 1)).astype(jnp.bfloat16)]
where the time goes in v1:
time: 367 us; the launch traced here: 365 us
  waiting for transfers between devices  158 us (43%)
  local copies, waits for them, and re-layouts  115 us (31%)
  starting transfers between devices  41.3 us (11%)
  other arithmetic  36.7 us (10%)
  between operations  14.1 us (4%)
    all_gather x3, waiting for transfers between devices, over_pieces(): blocks = lax.all_gather(array, axis)  155 us
    unnamed x53, local copies, waits for them, and re-layouts  57.9 us
    all_to_all x2, starting transfers between devices, copy_for_each(): return lax.all_to_all(copies, axis, split_axis=0, concat_axis=0, tiled=True)  15.3 us
    reshape x3, local copies, waits for them, and re-layouts, use_lots_all(): jnp.concatenate(lax.all_to_all(jnp.stack(jnp.split(original, lax.axis_siz...  14.4 us
    all_to_all x2, local copies, waits for them, and re-layouts, per_device(): lax.all_to_all(narrow_up, 'shard', split_axis=2, concat_axis=1, tiled=True)  13.6 us
    all_to_all x2, local copies, waits for them, and re-layouts, per_device(): lax.all_to_all(narrow_down, 'shard', split_axis=1, concat_axis=2, tiled=T...  13.6 us
    all_to_all x1, starting transfers between devices, per_device(): lax.all_to_all(narrow_down, 'shard', split_axis=1, concat_axis=2, tiled=T...  8.65 us
    all_to_all x1, starting transfers between devices, per_device(): lax.all_to_all(narrow_up, 'shard', split_axis=2, concat_axis=1, tiled=True)  8.63 us
  transfers between devices with their start and end apart: 8, of which 4 were waited for; matrix products, arithmetic and copies ran while one was open for 28% of the time, Pallas kernels for 0%

profile of v1, /device:TPU:6, one launch (start us, length us, event | category | flops | bytes accessed | tf_op | source)
XLA Modules:
  0.0 365.0 jit_solution(6633827243841249071)
XLA Ops:
  7.2 0.0 copy-start.2
  7.2 0.0 all-gather.7.cloned.1.call-start
  7.2 7.0 %copy.119 = f32[16,64,1024]{1,2,0:T(8,128)} copy(f32[16,64,1024]{2,1,0:T(8,128)} %param.8) | data formatting | bytes 8388608 | tf_op args[0]
  14.3 0.0 copy-done.2
  14.3 3.2 copy.118
  17.5 0.0 copy-start
  17.5 7.6 %abs_reduce_fusion = f32[16,1024]{1,0:T(8,128)} fusion(f32[16,64,1024]{1,2,0:T(8,128)} %copy.119, bf16[16,64,1024]{1,2,0:T(8,128)(2,1)} %copy.118), kind=kLoop, calls=%fused_computation.1 | loop fusion | flops 4177920 | bytes 6356992 | tf_op jit(solution)/shard_map/reduce_max | solution.py:41
  25.1 0.0 copy-start.3
  25.1 0.0 copy-start.4
  25.1 0.0 all-gather.7.cloned.1.call-update
  25.1 0.0 all-gather.9.cloned.1.call-start
  25.2 0.0 copy-done
  25.2 3.6 abs_reduce_fusion.2
  28.8 0.0 all-gather.9.cloned.1.call-update
  28.8 0.0 copy-done.3
  28.8 0.0 copy-done.4
  28.8 0.8 reshape.43
  29.6 11.1 %all-to-all-start.3 = ((bf16[32,2,512]{2,1,0:T(2,128)(2,1)}), bf16[32,2,512]{2,1,0:T(2,128)(2,1)S(1)}, u32[]{:S(2)}, u32[]{:S(2)}) async-start(bf16[32,2,512]{2,1,0:T(2,128)(2,1)} %reshape.43), calls=%async_computation.3 | async-start | bytes 131072 | tf_op jit(solution)/shard_map/all_to_all | solution.py:20
  40.7 0.0 all-gather.11.cloned.1.call-start
  40.7 4.3 %abs_reduce_fusion.1 = f32[16,1024]{1,0:T(8,128)} fusion(f32[16,1024,64]{1,2,0:T(8,128)} %param.12, bf16[16,1024,64]{1,2,0:T(8,128)(2,1)} %param.13), kind=kLoop, calls=%fused_computation.4 | loop fusion | flops 4177920 | bytes 6356992 | tf_op jit(solution)/shard_map/reduce_max | solution.py:43
  45.0 0.0 all-gather.11.cloned.1.call-update
  45.0 3.0 all-to-all-done.3
  48.0 0.1 reshape.44
  48.2 0.2 reshape.32
  48.4 0.7 broadcast_in_dim.5
  49.1 4.2 %all-to-all-start.4 = ((bf16[4,2048,16]{1,2,0:T(8,128)(2,1)}), bf16[4,2048,16]{1,2,0:T(8,128)(2,1)S(1)}, u32[]{:S(2)}, u32[]{:S(2)}) async-start(bf16[4,2048,16]{1,2,0:T(8,128)(2,1)} %broadcast_in_dim.5), calls=%async_computation.4 | async-start | bytes 524288 | tf_op jit(solution)/shard_map/all_to_all | solution.py:20
  53.3 43.3 %all-gather.7.cloned.1.call-done = f32[512,1024]{1,0:T(8,128)} async-done(((f32[16,1024]{1,0:T(8,128)}), f32[512,1024]{1,0:T(8,128)}) %all-gather.7.cloned.1.call-update) | async-done | bytes 2097168 | tf_op jit(solution)/shard_map/all_gather | solution.py:8
  96.6 1.7 reduce_max.55
  98.3 6.1 %divide_convert_fusion = bf16[16,64,1024]{1,2,0:T(8,128)(2,1)S(1)} fusion(f32[16,64,1024]{1,2,0:T(8,128)} %copy.119, bf16[16,64,1024]{1,2,0:T(8,128)(2,1)} %copy.118, f32[16,1024]{1,0:T(8,128)S(1)} %reduce_max.55), kind=kLoop, calls=%fused_computation | loop fusion | flops 4194304 | bytes 8454144 | tf_op jit(solution)/shard_map/convert_element_type | solution.py:46
  105.3 0.0 copy-start.1
  105.3 1.9 copy-done.1
  107.3 7.9 %reshape.37 = bf16[32,2,16384]{2,1,0:T(2,128)(2,1)} reshape(bf16[32,16,32,64]{3,2,1,0:T(8,128)(2,1)} %bitcast.168) | data formatting | bytes 4194304
  115.1 0.0 all-to-all-done.4
  115.1 8.6 %all-to-all-start = ((bf16[32,2,16384]{2,1,0:T(2,128)(2,1)}), bf16[32,2,16384]{2,1,0:T(2,128)(2,1)S(1)}, u32[]{:S(2)}, u32[]{:S(2)}) async-start(bf16[32,2,16384]{2,1,0:T(2,128)(2,1)} %reshape.37), calls=%async_computation | async-start | bytes 4194304 | tf_op jit(solution)/shard_map/all_to_all | solution.py:53
  123.7 56.0 %all-gather.9.cloned.1.call-done = f32[512,1024]{1,0:T(8,128)} async-done(((f32[16,1024]{1,0:T(8,128)}), f32[512,1024]{1,0:T(8,128)}) %all-gather.9.cloned.1.call-update) | async-done | bytes 2097168 | tf_op jit(solution)/shard_map/all_gather | solution.py:8
  179.7 1.7 reduce_max.57
  181.4 5.0 %divide_convert_fusion.2 = bf16[16,64,1024]{2,1,0:T(8,128)(2,1)} fusion(f32[16,64,1024]{2,1,0:T(8,128)} %param.10, bf16[16,64,1024]{2,1,0:T(8,128)(2,1)} %param.11, f32[16,1024]{1,0:T(8,128)S(1)} %reduce_max.57), kind=kLoop, calls=%fused_computation.6 | loop fusion | flops 4194304 | bytes 8454144 | tf_op jit(solution)/shard_map/convert_element_type | solution.py:47
  186.4 6.2 %copy.123 = bf16[16,64,1024]{1,0,2:T(8,128)(2,1)} copy(bf16[16,64,1024]{2,1,0:T(8,128)(2,1)} %divide_convert_fusion.2) | data formatting | bytes 4194304 | tf_op jit(solution)/shard_map/convert_element_type | solution.py:47
  192.6 7.9 %reshape.39 = bf16[32,2,16384]{2,1,0:T(2,128)(2,1)} reshape(bf16[1024,16,64]{2,1,0:T(8,128)(2,1)} %bitcast.164) | data formatting | bytes 4194304
  200.5 0.0 all-to-all-done
  200.5 8.6 %all-to-all-start.1 = ((bf16[32,2,16384]{2,1,0:T(2,128)(2,1)}), bf16[32,2,16384]{2,1,0:T(2,128)(2,1)}, u32[]{:S(2)}, u32[]{:S(2)}) async-start(bf16[32,2,16384]{2,1,0:T(2,128)(2,1)} %reshape.39), calls=%async_computation.1 | async-start | bytes 4194304 | tf_op jit(solution)/shard_map/all_to_all | solution.py:64
  209.1 55.8 %all-gather.11.cloned.1.call-done = f32[512,1024]{1,0:T(8,128)} async-done(((f32[16,1024]{1,0:T(8,128)}), f32[512,1024]{1,0:T(8,128)}) %all-gather.11.cloned.1.call-update) | async-done | bytes 2097168 | tf_op jit(solution)/shard_map/all_gather | solution.py:8
  264.9 1.7 reduce_max.59
  266.6 5.0 %divide_convert_fusion.1 = bf16[16,1024,64]{1,2,0:T(8,128)(2,1)} fusion(f32[16,1024,64]{1,2,0:T(8,128)} %param.12, bf16[16,1024,64]{1,2,0:T(8,128)(2,1)} %param.13, f32[16,1024]{1,0:T(8,128)S(1)} %reduce_max.59), kind=kLoop, calls=%fused_computation.3 | loop fusion | flops 4194304 | bytes 8454144 | tf_op jit(solution)/shard_map/convert_element_type | solution.py:48
  271.6 6.2 %copy.128 = bf16[16,1024,64]{2,0,1:T(8,128)(2,1)} copy(bf16[16,1024,64]{1,2,0:T(8,128)(2,1)} %divide_convert_fusion.1) | data formatting | bytes 4194304 | tf_op jit(solution)/shard_map/convert_element_type | solution.py:48
  277.8 7.9 %reshape.41 = bf16[32,2,16384]{2,1,0:T(2,128)(2,1)} reshape(bf16[1024,16,64]{2,1,0:T(8,128)(2,1)} %bitcast.165) | data formatting | bytes 4194304
  285.6 0.0 all-to-all-done.1
  285.6 8.6 %all-to-all-start.2 = ((bf16[32,2,16384]{2,1,0:T(2,128)(2,1)}), bf16[32,2,16384]{2,1,0:T(2,128)(2,1)}, u32[]{:S(2)}, u32[]{:S(2)}) async-start(bf16[32,2,16384]{2,1,0:T(2,128)(2,1)} %reshape.41), calls=%async_computation.2 | async-start | bytes 4194304 | tf_op jit(solution)/shard_map/all_to_all | solution.py:66
  294.3 0.7 constant_dynamic-slice_fusion.2
  295.0 0.7 constant_dynamic-slice_fusion
  295.7 0.7 constant_dynamic-slice_fusion.1
  296.3 4.0 %reshape.38 = bf16[32,16,32,64]{3,2,1,0:T(8,128)(2,1)} reshape(bf16[32,2,16384]{2,1,0:T(2,128)(2,1)S(1)} %all-to-all-done) | data formatting | bytes 4194304
  300.3 3.0 bitcast_bitcast_fusion
  303.3 4.6 %copy.120 = bf16[16,32,64,32]{2,1,3,0:T(8,128)(2,1)} copy(bf16[16,32,64,32]{2,3,0,1:T(8,128)(2,1)S(1)} %bitcast_bitcast_fusion) | data formatting | bytes 4194304 | tf_op jit(solution)/shard_map/reshape | solution.py:52
  308.0 6.7 %reshape.31 = bf16[16,2048,32]{1,2,0:T(8,128)(2,1)} reshape(bf16[16,32,64,32]{2,1,3,0:T(8,128)(2,1)} %copy.120) | data formatting | bytes 4194304 | tf_op jit(solution)/shard_map/reshape | solution.py:52
  314.7 7.9 %reshape.40 = bf16[1024,16,64]{2,1,0:T(8,128)(2,1)} reshape(bf16[32,2,16384]{2,1,0:T(2,128)(2,1)} %all-to-all-done.1) | data formatting | bytes 4194304
  322.6 6.9 %copy.125 = bf16[16,32,64,32]{2,1,3,0:T(8,128)(2,1)} copy(bf16[16,32,64,32]{2,0,3,1:T(8,128)(2,1)} %bitcast.166) | data formatting | bytes 4194304 | tf_op jit(solution)/shard_map/all_to_all | solution.py:64
  329.5 6.7 %all_to_all.39 = bf16[16,2048,32]{1,2,0:T(8,128)(2,1)} reshape(bf16[16,32,64,32]{2,1,3,0:T(8,128)(2,1)} %copy.125) | data formatting | bytes 4194304 | tf_op jit(solution)/shard_map/all_to_all | solution.py:64
  336.2 0.0 all-to-all-done.2
  336.2 7.9 %reshape.42 = bf16[1024,16,64]{2,1,0:T(8,128)(2,1)} reshape(bf16[32,2,16384]{2,1,0:T(2,128)(2,1)} %all-to-all-done.2) | data formatting | bytes 4194304
  344.2 6.9 %copy.130 = bf16[16,32,32,64]{3,2,1,0:T(8,128)(2,1)} copy(bf16[16,32,32,64]{3,0,1,2:T(8,128)(2,1)} %bitcast.167) | data formatting | bytes 4194304 | tf_op jit(solution)/shard_map/all_to_all | solution.py:66
  351.0 6.7 %all_to_all.43 = bf16[16,32,2048]{2,1,0:T(8,128)(2,1)} reshape(bf16[16,32,32,64]{3,2,1,0:T(8,128)(2,1)} %copy.130) | data formatting | bytes 4194304 | tf_op jit(solution)/shard_map/all_to_all | solution.py:66
  357.8 0.7 copy.168
  (35 shorter events, 0.7 us)
Async XLA Ops:
  7.2 7.1 %copy-start.2 = (bf16[16,64,1024]{2,1,0:T(8,128)(2,1)S(1)}, bf16[16,64,1024]{2,1,0:T(8,128)(2,1)}, u32[]{:S(2)}) copy-start(bf16[16,64,1024]{2,1,0:T(8,128)(2,1)} %param.9) | copy-start | bytes 6291460
  7.2 89.4 %all-gather.7.cloned.1.call-start = ((), (), s32[]{:S(2)}) async-start(), calls=%async_computation.5 | async-start | bytes 2162688 | tf_op jit(solution)/shard_map/all_gather | solution.py:8
  17.5 7.7 %copy-start = (bf16[16,64,1024]{2,1,0:T(8,128)(2,1)S(1)}, bf16[16,64,1024]{2,1,0:T(8,128)(2,1)}, u32[]{:S(2)}) copy-start(bf16[16,64,1024]{2,1,0:T(8,128)(2,1)} %param.11) | copy-start | bytes 6291460
  25.1 3.7 %copy-start.3 = (f32[64,16]{0,1:T(8,128)S(1)}, f32[64,16]{0,1:T(8,128)}, u32[]{:S(2)}) copy-start(f32[64,16]{0,1:T(8,128)} %param.14) | copy-start | bytes 12292
  25.1 3.7 %copy-start.4 = (f32[64]{0:T(128)S(1)}, f32[64]{0:T(128)}, u32[]{:S(2)}) copy-start(f32[64]{0:T(128)} %param.15) | copy-start | bytes 772
  25.1 154.6 %all-gather.9.cloned.1.call-start = ((), (), s32[]{:S(2)}) async-start(), calls=%async_computation.6 | async-start | bytes 2162688 | tf_op jit(solution)/shard_map/all_gather | solution.py:8
  29.6 18.4 %all-to-all-start.3 = ((bf16[32,2,512]{2,1,0:T(2,128)(2,1)}), bf16[32,2,512]{2,1,0:T(2,128)(2,1)S(1)}, u32[]{:S(2)}, u32[]{:S(2)}) async-start(bf16[32,2,512]{2,1,0:T(2,128)(2,1)} %reshape.43), calls=%async_computation.3 | async-start | bytes 131072 | tf_op jit(solution)/shard_map/all_to_all | solution.py:20
  40.7 224.2 %all-gather.11.cloned.1.call-start = ((), (), s32[]{:S(2)}) async-start(), calls=%async_computation.7 | async-start | bytes 2162688 | tf_op jit(solution)/shard_map/all_gather | solution.py:8
  49.1 66.0 %all-to-all-start.4 = ((bf16[4,2048,16]{1,2,0:T(8,128)(2,1)}), bf16[4,2048,16]{1,2,0:T(8,128)(2,1)S(1)}, u32[]{:S(2)}, u32[]{:S(2)}) async-start(bf16[4,2048,16]{1,2,0:T(8,128)(2,1)} %broadcast_in_dim.5), calls=%async_computation.4 | async-start | bytes 524288 | tf_op jit(solution)/shard_map/all_to_all | solution.py:20
  105.3 1.9 copy-start.1
  115.1 85.3 %all-to-all-start = ((bf16[32,2,16384]{2,1,0:T(2,128)(2,1)}), bf16[32,2,16384]{2,1,0:T(2,128)(2,1)S(1)}, u32[]{:S(2)}, u32[]{:S(2)}) async-start(bf16[32,2,16384]{2,1,0:T(2,128)(2,1)} %reshape.37), calls=%async_computation | async-start | bytes 4194304 | tf_op jit(solution)/shard_map/all_to_all | solution.py:53
  200.5 85.2 %all-to-all-start.1 = ((bf16[32,2,16384]{2,1,0:T(2,128)(2,1)}), bf16[32,2,16384]{2,1,0:T(2,128)(2,1)}, u32[]{:S(2)}, u32[]{:S(2)}) async-start(bf16[32,2,16384]{2,1,0:T(2,128)(2,1)} %reshape.39), calls=%async_computation.1 | async-start | bytes 4194304 | tf_op jit(solution)/shard_map/all_to_all | solution.py:64
  285.6 50.6 %all-to-all-start.2 = ((bf16[32,2,16384]{2,1,0:T(2,128)(2,1)}), bf16[32,2,16384]{2,1,0:T(2,128)(2,1)}, u32[]{:S(2)}, u32[]{:S(2)}) async-start(bf16[32,2,16384]{2,1,0:T(2,128)(2,1)} %reshape.41), calls=%async_computation.2 | async-start | bytes 4194304 | tf_op jit(solution)/shard_map/all_to_all | solution.py:66
Sparse Core Ops, SparseCore 0:
  25.2 71.2 all-gather.6
  100.2 79.4 all-gather.8
  183.4 81.4 all-gather.10
